TPU v7x, 256 devices: a whole 4x4x8 slice. The times are simulated.
256 devices in a mesh: rep: 2 (over y_hi), fsdp: 128 (over z, x, y_lo, core).
Axes of the slice: x: 4, y: 4 (y_hi: 2, y_lo: 2; y = y_hi * 2 + y_lo), z: 8, core: 2. Of those that a mesh axis runs over, the one named last changes fastest.
Arguments:
- tokens: bfloat16 [131072, 4096], P(('rep', 'fsdp')), may hold values from -24 to 24
- value_cot: bfloat16 [131072, 1024], P(('rep', 'fsdp')), may hold values from -6 to 6
- value_weight: bfloat16 [2, 4096, 1024], P('rep', 'fsdp'), may hold values from -0.09375 to 0.09375
- global_params: float32 [16777216], P('fsdp'), may hold values from -6 to 6
- local_params: float32 [2, 16777216], P('rep', 'fsdp'), may hold values from -6 to 6
- momentum: float32 [16777216], P('fsdp'), may hold values from -3 to 3
Outputs:
- token_grad: bfloat16 [131072, 4096], P(('rep', 'fsdp'))
- value_grad: float32 [2, 4096, 1024], P('rep', 'fsdp')
- new_global: float32 [16777216], P('fsdp')
- new_moment: float32 [16777216], P('fsdp')
All inputs are finite; a program needn't handle non-finite values.
Results may differ from a plain program's by a relative error of at most 0.001.
Values may be sent and summed in bfloat16 or wider, within the bound.
A program may use at most 128 MiB of HBM per device.

v0:
```python
import jax
import jax.numpy as jnp
from jax import lax
from jax.sharding import Mesh
from jax.sharding import PartitionSpec as P

FSDP = ("fsdp_0", "fsdp_1", "fsdp_2", "fsdp_3")
REP_FSDP = ("rep", "fsdp_0", "fsdp_1", "fsdp_2", "fsdp_3")


def split_up(x, dim, length):
    before, after = (x.shape[:dim], x.shape[dim + 1 :])
    return jnp.moveaxis(x.reshape(*before, length, -1, *after), dim, 0)


def summed_rows(x, chips, core, dim):
    sizes = (lax.axis_size(chips), lax.axis_size(core))
    tiles = split_up(x, dim, sizes[0] * sizes[1])
    inside = tiles.shape[1:]
    tiles = tiles.reshape(*sizes, *inside).swapaxes(0, 1).reshape(-1, *inside)
    tiles = lax.psum_scatter(tiles, core, scatter_dimension=0, tiled=True)
    return lax.psum_scatter(tiles, chips, scatter_dimension=0, tiled=True)[0]


def copy_for_each(x, axis):
    length = lax.axis_size(axis)
    return lax.all_to_all(jnp.broadcast_to(x[None], (length, *x.shape)), axis, 0, 0, tiled=True)


def over_copies(x, axis):
    everything = copy_for_each(x, axis)
    return jnp.sum(everything, axis=0)


def grad_term(tokens, columns):
    return lax.dot_general(
        tokens, columns, (((0,), (0,)), ((), ())), preferred_element_type=jnp.float32
    )


def shards(tokens, value_cot, value_weight, global_params, local_params, momentum):
    weight = value_weight[0]
    token_grad = lax.dot_general(
        value_cot,
        lax.all_gather(weight, FSDP, axis=0, tiled=True),
        (((1,), (1,)), ((), ())),
        preferred_element_type=jnp.float32,
    ).astype(jnp.bfloat16)
    groups = lax.axis_size(FSDP)
    factor = 1.0 / jnp.sqrt(jnp.float32(tokens.shape[0] * groups))
    summed = summed_rows(grad_term(tokens, value_cot), ("fsdp_0", "fsdp_1", "fsdp_2"), "fsdp_3", 0)
    value_grad = (summed * factor)[None]
    totals = over_copies(local_params[0], "rep")
    pseudo = global_params - totals / lax.axis_size("rep")
    new_moment = 0.9 * momentum + pseudo
    new_global = global_params - 0.7 * (pseudo + 0.9 * new_moment)
    return (token_grad, value_grad, new_global, new_moment)


def solution(mesh):
    split = Mesh(
        mesh.devices.reshape(mesh.shape["rep"], 8, 4, 2, 2),
        ("rep", "fsdp_0", "fsdp_1", "fsdp_2", "fsdp_3"),
    )
    return jax.shard_map(
        shards,
        mesh=split,
        in_specs=(
            P(REP_FSDP, None),
            P(REP_FSDP, None),
            P("rep", FSDP, None),
            P(FSDP),
            P("rep", FSDP),
            P(FSDP),
        ),
        out_specs=(P(REP_FSDP, None), P("rep", FSDP, None), P(FSDP), P(FSDP)),
        check_vma=False,
    )
```

profile of v0, /device:TPU:16, one launch (start us, length us, event | category | flops | bytes accessed | tf_op | source)
XLA Modules:
  0.0 405.7 jit_solution(8462821204067004481)
XLA Ops:
  8.0 0.0 copy-start
  8.0 0.0 reduce-scatter.3.cloned.1.call-start
  8.1 1.2 copy-done
  9.2 6.5 %fusion.5 = f32[4096,1024]{1,0:T(8,128)S(1)} fusion(bf16[512,4096]{1,0:T(8,128)(2,1)} %param.6, bf16[512,1024]{1,0:T(8,128)(2,1)S(1)} %copy-done), kind=kOutput, calls=%fused_computation.7 | convolution fusion | flops 4294967296 | bytes 22020096 | tf_op jit(solution)/shard_map/dot_general | solution.py:36
  15.7 6.1 %copy.12 = f32[2,64,32,1024]{3,2,1,0:T(8,128)} copy(f32[2,64,32,1024]{3,2,0,1:T(8,128)S(1)} %bitcast.14) | data formatting | bytes 33554432 | tf_op jit(solution)/shard_map/transpose | solution.py:20
  21.8 0.0 reduce-scatter.3.cloned.1.call-update
  21.8 0.0 copy-start.1
  21.8 0.0 copy-start.2
  21.8 0.0 all-gather.3.cloned.1.call-start
  21.9 0.5 all-gather.3.cloned.1.call-update
  22.4 0.0 reduce-scatter.5.cloned.1.call-start
  22.5 32.8 %reduce-scatter.3.cloned.1.call-done = f32[64,32,1024]{2,1,0:T(8,128)} async-done(((f32[128,32,1024]{2,1,0:T(8,128)}), f32[64,32,1024]{2,1,0:T(8,128)}) %reduce-scatter.3.cloned.1.call-update) | async-done | bytes 8388624 | tf_op jit(solution)/shard_map/reduce_scatter | solution.py:21
  55.3 0.0 reduce-scatter.5.cloned.1.call-update
  55.3 0.0 copy-done.1
  55.3 0.5 broadcast_in_dim.2
  55.9 19.6 %all_to_all.6 = f32[2,1,131072]{2,1,0:T(1,128)S(1)} all-to-all(f32[2,1,131072]{2,1,0:T(1,128)S(1)} %broadcast_in_dim.2), channel_id=1, replica_groups=mesh['rep'=2,'fsdp_0'=8,'fsdp_1'=4,'fsdp_2'=2,'fsdp_3'=2] {'rep'}, dimensions={0} | all-to-all | bytes 2097152 | tf_op jit(solution)/shard_map/all_to_all | solution.py:27
  75.4 1.5 reduce_sum.9
  76.9 0.0 copy-done.2
  76.9 2.1 multiply_subtract_fusion
  79.1 173.3 %all-gather.3.cloned.1.call-done = bf16[1,4096,1024]{2,1,0:T(8,128)(2,1)} async-done(((bf16[1,32,1024]{2,1,0:T(8,128)(2,1)}), bf16[1,4096,1024]{2,1,0:T(8,128)(2,1)}) %all-gather.3.cloned.1.call-update) | async-done | bytes 8388624 | tf_op jit(solution)/shard_map/all_gather | solution.py:45
  252.4 9.5 %fusion.2 = bf16[512,4096]{1,0:T(8,128)(2,1)} fusion(bf16[512,1024]{1,0:T(8,128)(2,1)S(1)} %copy-done, bf16[1,4096,1024]{2,1,0:T(8,128)(2,1)} %all-gather.3.cloned.1.call-done), kind=kOutput, calls=%fused_computation.2 | convolution fusion | flops 4297064448 | bytes 13631488 | tf_op jit(solution)/shard_map/dot_general | solution.py:43
  261.9 134.8 %reduce-scatter.5.cloned.1.call-done = f32[1,32,1024]{2,1,0:T(8,128)} async-done(((f32[64,32,1024]{2,1,0:T(8,128)}), f32[1,32,1024]{2,1,0:T(8,128)}) %reduce-scatter.5.cloned.1.call-update) | async-done | bytes 131088 | tf_op jit(solution)/shard_map/reduce_scatter | solution.py:22
  396.7 1.6 broadcast_multiply_fusion
Async XLA Ops:
  8.0 1.2 copy-start
  8.0 47.3 %reduce-scatter.3.cloned.1.call-start = ((), (), s32[]{:S(2)}) async-start(), calls=%async_computation.3 | async-start | bytes 25165824 | tf_op jit(solution)/shard_map/reduce_scatter | solution.py:21
  21.8 33.5 %copy-start.1 = (f32[1,131072]{1,0:T(1,128)S(1)}, f32[1,131072]{1,0:T(1,128)}, u32[]{:S(2)}) copy-start(f32[1,131072]{1,0:T(1,128)} %param.10) | copy-start | bytes 1572868
  21.8 55.1 %copy-start.2 = (f32[131072]{0:T(1024)S(1)}, f32[131072]{0:T(1024)}, u32[]{:S(2)}) copy-start(f32[131072]{0:T(1024)} %param.9) | copy-start | bytes 1572868
  21.8 230.5 %all-gather.3.cloned.1.call-start = ((), (), s32[]{:S(2)}) async-start(), calls=%async_computation.5 | async-start | bytes 8454144 | tf_op jit(solution)/shard_map/all_gather | solution.py:45
  22.4 374.3 %reduce-scatter.5.cloned.1.call-start = ((), (), s32[]{:S(2)}) async-start(), calls=%async_computation.4 | async-start | bytes 8519680 | tf_op jit(solution)/shard_map/reduce_scatter | solution.py:22
Sparse Core Ops, SparseCore 0:
  21.9 33.3 reduce-scatter.2
  57.8 338.8 reduce-scatter.4
Sparse Core Ops, SparseCore 1:
  24.2 228.1 all-gather.2
where the time goes:
time: 406 us
  waiting for transfers between devices  341 us (84%)
  blocking collectives  19.6 us (5%)
  matrix products  16 us (4%)
  between operations  15.5 us (4%)
  local copies, waits for them, and re-layouts  7.79 us (2%)
  other arithmetic  5.2 us (1%)
    all_gather x1, waiting for transfers between devices, shards(): lax.all_gather(weight, FSDP, axis=0, tiled=True)  173 us
    reduce_scatter x1, waiting for transfers between devices, summed_rows(): return lax.psum_scatter(tiles, chips, scatter_dimension=0, tiled=True)[0]  135 us
    reduce_scatter x1, waiting for transfers between devices, summed_rows(): tiles = lax.psum_scatter(tiles, core, scatter_dimension=0, tiled=True)  32.8 us
    all_to_all x1, blocking collectives, copy_for_each(): lax.all_to_all(jnp.broadcast_to(x[None], (length, *x.shape)), axis, 0, 0,...  19.6 us
    dot_general x1, matrix products, shards(): lax.dot_general(value_cot, lax.all_gather(weight, FSDP, axis=0, tiled=Tru...  9.49 us
  transfers between devices with their start and end apart: 3, of which 3 were waited for; matrix products, arithmetic and copies ran while one was open for 3% of the time, Pallas kernels for 0%

commit v1 on v0

v1 whole, which is shorter than its diff:
```python
import functools

import jax
import jax.numpy as jnp
from jax import lax
from jax.experimental import pallas as pl
from jax.experimental.pallas import tpu as pltpu
from jax.sharding import Mesh
from jax.sharding import PartitionSpec as P

MESH_ID = pl.DeviceIdType.MESH
AXES = ("rep", "z", "x", "y", "c")
FSDP = AXES[1:]
SIZES = {"z": 8, "x": 4, "y": 2}
ROWS = 32
LANES = 128

RS_ORDERS = ("zxy", "xzy", "yzx", "zxy", "xyz", "yxz", "zyx", "xyz")
AG_CHUNKS = ((0, 2, "xyz"), (2, 1, "zyx"), (3, 1, "zxy"), (4, 2, "zyx"), (6, 1, "xyz"), (7, 1, "zxy"))
PLANES = (4, 5, 3, 6, 2, 7, 1, 0)

SCALE = 2.0 ** -6
LOW = 2.0 ** -8
HIGH = 2.0 ** 8


def encode(v):
    u = v * SCALE
    a = jnp.abs(u)
    p = a * jnp.clip(a, LOW, HIGH)
    p = p * p
    p = p * p
    return jnp.where(u < 0, -p, p).astype(jnp.bfloat16)


def decode(coded):
    y = coded.astype(jnp.float32)
    a = jnp.abs(y)
    r = jnp.sqrt(jnp.sqrt(a))
    m = jnp.sqrt(r)
    v = jnp.where(a < LOW**8, r * (1.0 / LOW), jnp.where(a > HIGH**8, r * (1.0 / HIGH), m))
    v = v * (1.0 / SCALE)
    return jnp.where(y < 0, -v, v)


def arms(n, flip):
    if n == 2:
        return ((1, 1),)
    long, short = n // 2, n - 1 - n // 2
    return ((1, long), (-1, short)) if flip else ((1, short), (-1, long))


def link(dim, sign):
    return dim if SIZES[dim] == 2 else dim + ("+" if sign > 0 else "-")


class Plan:
    RATE = 44e3
    HOP = 2.3

    def __init__(self):
        self.order = []
        self.tc = 0.0
        self.links = {}
        self.ready = []
        self.serial = 0
        self.run()

    def send(self, name, size, rate=None, hop=None):
        begin = max(self.links.get(name, 0.0), self.tc)
        self.links[name] = begin + size / (rate or self.RATE)
        return self.links[name] + (hop or self.HOP)

    def add(self, time, priority, event, duration):
        self.ready.append([time, priority, self.serial, event, duration])
        self.serial += 1

    def rs_nb(self, q, k):
        n = 1
        for d in RS_ORDERS[q][k + 1 :]:
            n *= SIZES[d]
        return n

    def rs_send(self, q, k, sign, j):
        nb = self.rs_nb(q, k)
        d = RS_ORDERS[q][k]
        length = dict(arms(SIZES[d], q % 2))[sign]
        at = self.send(link(d, sign), nb * ROWS * LANES * 2)
        if j + 1 < length:
            self.add(at, 0, ("rs", q, k, sign, j), 0.1 + 0.03 * nb)
        else:
            got = self.last.setdefault((q, k), {})
            got[sign] = at
            if len(got) == len(arms(SIZES[d], q % 2)):
                self.add(max(got.values()), 0, ("fin", q, k), 0.2 + 0.06 * nb)

    def ag_bytes(self, i, k):
        _, tiles, order = AG_CHUNKS[i]
        n = 1
        for d in order[:k]:
            n *= SIZES[d]
        return n * ROWS * LANES * tiles * 2

    def ag_send(self, i, k, sign, j):
        d = AG_CHUNKS[i][2][k]
        at = self.send(link(d, sign), self.ag_bytes(i, k))
        self.add(at, 0, ("ag", i, k, sign, j), 0.03)

    def ag_phase(self, i, k):
        d = AG_CHUNKS[i][2][k]
        for sign, _ in arms(SIZES[d], i % 2):
            self.ag_send(i, k, sign, 0)

    def run(self):
        self.last = {}
        self.tc = 2.0
        self.add(2.0, 0, ("start",), 0.1)
        for n in range(len(PLANES)):
            self.add(3.0, 2 + n, ("mm", n), 0.9)
        seen = {}
        planes = {}
        left = sum(len(AG_CHUNKS) * [sum(s - 1 for s in SIZES.values())])
        while self.ready:
            now = [r for r in self.ready if r[0] <= self.tc]
            if now:
                pick = min(now, key=lambda r: (r[1], r[0], r[2]))
            else:
                pick = min(self.ready, key=lambda r: (r[0], r[1], r[2]))
            self.ready.remove(pick)
            event = pick[3]
            self.tc = max(self.tc, pick[0]) + pick[4]
            self.order.append(event)
            kind = event[0]
            if kind == "start":
                for i in range(len(AG_CHUNKS)):
                    self.ag_phase(i, 0)
                self.add(self.send("y", 524288), 1, ("relay",), 0.05)
            elif kind == "relay":
                self.add(self.send("cross", 524288), 1, ("outer",), 0.6)
            elif kind == "mm":
                planes[PLANES[event[1]]] = self.send("core", 1 << 20, 6e5, 1.0)
                n_all = len(planes) == len(PLANES)
                for q, order in enumerate(RS_ORDERS):
                    for sign, length in arms(SIZES[order[0]], q % 2):
                        if order[0] == "z":
                            if (sign * length) % SIZES["z"] == PLANES[event[1]]:
                                self.add(planes[PLANES[event[1]]], 1, ("go", q, sign), 0.4)
                        elif n_all:
                            self.add(max(planes.values()), 1, ("go", q, sign), 0.1 + 0.03 * self.rs_nb(q, 0))
            elif kind == "go":
                self.rs_send(event[1], 0, event[2], 0)
            elif kind == "rs":
                _, q, k, sign, j = event
                self.rs_send(q, k, sign, j + 1)
            elif kind == "fin":
                _, q, k = event
                if k < 2:
                    for sign, _ in arms(SIZES[RS_ORDERS[q][k + 1]], q % 2):
                        self.rs_send(q, k + 1, sign, 0)
            elif kind == "ag":
                _, i, k, sign, j = event
                d = AG_CHUNKS[i][2][k]
                self.send("core", self.ag_bytes(i, k), 6e5, 1.0)
                if j + 1 < dict(arms(SIZES[d], i % 2))[sign]:
                    self.ag_send(i, k, sign, j + 1)
                seen[i, k] = seen.get((i, k), 0) + 1
                left -= 1
                if seen[i, k] == SIZES[d] - 1 and k < 2:
                    self.ag_phase(i, k + 1)
                if not left:
                    for z in range(SIZES["z"]):
                        self.add(self.tc + 3.0, 3, ("tg", z), 0.9)


def kernel(plan, factor, x_hbm, cot_hbm, w_hbm, g_hbm, l_hbm, m_hbm, tg_hbm, vg_hbm, ng_hbm, nm_hbm,
           xs, cs, w, pb, pp, got, put, tg, vg, g, l, m, mid, other, ng, nm,
           in_sem, out_sem, ag_s, ag_r, fw_s, fw_r, pp_s, pp_r, rs_s, rs_r, rep_s, rep_r):
    at = {name: lax.axis_index(name) for name in AXES}
    me_c = at["c"]

    def peer(**moved):
        return tuple(moved.get(name, at[name]) for name in AXES)

    def towards(dim, sign):
        n = SIZES[dim]
        return peer(**{dim: lax.rem(at[dim] + (sign + n), n)})

    def shifted(dim, by):
        n = SIZES[dim]
        return lax.rem(at[dim] + (by % n), n)

    core = peer(c=1 - me_c)
    across = peer(rep=1 - at["rep"], y=1 - at["y"])
    peers = [core, across]
    for dim in SIZES:
        peers += [towards(dim, sign) for sign, _ in arms(SIZES[dim], 0)]

    local = [
        pltpu.make_async_copy(w_hbm, w.at[at["z"], at["x"], at["y"], me_c], in_sem.at[0]),
        pltpu.make_async_copy(cot_hbm, cs, in_sem.at[1]),
        pltpu.make_async_copy(l_hbm, l, in_sem.at[3]),
        pltpu.make_async_copy(x_hbm, xs, in_sem.at[2]),
        pltpu.make_async_copy(g_hbm, g, in_sem.at[4]),
        pltpu.make_async_copy(m_hbm, m, in_sem.at[5]),
    ]
    for copy in local:
        copy.start()
    barrier = pltpu.get_barrier_semaphore()
    for device in peers:
        pl.semaphore_signal(barrier, inc=1, device_id=device, device_id_type=MESH_ID)
    pl.semaphore_wait(barrier, len(peers))

    def remote(src, dst, send, recv, device):
        return pltpu.make_async_remote_copy(
            src_ref=src, dst_ref=dst, send_sem=send, recv_sem=recv, device_id=device, device_id_type=MESH_ID
        )

    ag_copies, rs_copies, rs_slot = {}, {}, {}
    used = {"ag": 0, "rs": 0, "block": 0}

    def ag_region(i, k, sign, j):
        tile, tiles, order = AG_CHUNKS[i]
        index = {d: slice(None) for d in order[:k]}
        index[order[k]] = shifted(order[k], -sign * j)
        for d in order[k + 1 :]:
            index[d] = at[d]
        return w.at[index["z"], index["x"], index["y"], me_c, :, pl.ds(tile * LANES, tiles * LANES)]

    def ag_send(i, k, sign, j):
        n = used["ag"]
        used["ag"] += 1
        region = ag_region(i, k, sign, j)
        copy = remote(region, region, ag_s.at[n], ag_r.at[n], towards(AG_CHUNKS[i][2][k], sign))
        copy.start()
        ag_copies[i, k, sign, j] = copy

    def ag_phase(i, k):
        for sign, _ in arms(SIZES[AG_CHUNKS[i][2][k]], i % 2):
            ag_send(i, k, sign, 0)

    def nb_of(q, k):
        n = 1
        for d in RS_ORDERS[q][k + 1 :]:
            n *= SIZES[d]
        return n

    def pieces(q, k, dest):
        order = RS_ORDERS[q]
        index = {d: at[d] for d in order[:k]}
        index[order[k]] = dest
        free = sorted(order[k + 1 :], key="zxy".index)
        if not free:
            yield dict(index), 0, 1
        elif len(free) == 1 and SIZES[free[0]] <= 4:
            n = SIZES[free[0]]
            yield {**index, free[0]: slice(None)}, 0, n
        elif len(free) == 1:
            n = SIZES[free[0]]
            for h in range(n // 4):
                yield {**index, free[0]: pl.ds(4 * h, 4)}, 4 * h, 4
        else:
            inner = SIZES[free[1]]
            for o in range(SIZES[free[0]]):
                yield {**index, free[0]: o, free[1]: slice(None)}, o * inner, inner

    def cols(q):
        return pl.ds(q * LANES, LANES)

    def own(q, k, index, n):
        v = pb[index["z"], index["x"], index["y"], me_c, :, cols(q)].reshape(n, ROWS, LANES)
        if k == 0:
            v = v + pp[index["z"], index["x"], index["y"], :, cols(q)].reshape(n, ROWS, LANES)
        return v

    def rs_send(q, k, sign, j):
        d = RS_ORDERS[q][k]
        length = dict(arms(SIZES[d], q % 2))[sign]
        nb = nb_of(q, k)
        base = used["block"]
        used["block"] += nb
        n = used["rs"]
        used["rs"] += 1
        before = rs_slot.get((q, k, sign, j - 1))
        for index, first, count in pieces(q, k, shifted(d, sign * (length - j))):
            v = own(q, k, index, count)
            if before is not None:
                v = v + decode(got[before + first : before + first + count])
            put[base + first : base + first + count] = encode(v)
        copy = remote(put.at[pl.ds(base, nb)], got.at[pl.ds(base, nb)], rs_s.at[n], rs_r.at[n], towards(d, sign))
        copy.start()
        rs_copies[q, k, sign, j] = copy
        rs_slot[q, k, sign, j] = base

    plane_copies = {}
    plane_seen = set()

    def plane_wait(offset):
        if offset not in plane_seen:
            plane_seen.add(offset)
            plane_copies[offset].wait_recv()

    ag_seen = {}
    outs = []
    gathered = [False]
    forwarded = w.at[:, :, :, me_c]
    everything = remote(forwarded, forwarded, fw_s, fw_r, core)
    hop1 = remote(l, mid, rep_s.at[0], rep_r.at[0], towards("y", 1))
    hop2 = remote(mid, other, rep_s.at[1], rep_r.at[1], across)

    for event in plan.order:
        kind = event[0]
        if kind == "start":
            local[0].wait()
            for i in range(len(AG_CHUNKS)):
                ag_phase(i, 0)
            mine = w.at[at["z"], at["x"], at["y"], me_c]
            remote(mine, mine, fw_s, fw_r, core).start()
            local[2].wait()
            hop1.start()
            local[1].wait()
            local[3].wait()
        elif kind == "relay":
            hop1.wait_recv()
            hop2.start()
        elif kind == "outer":
            local[4].wait()
            local[5].wait()
            hop2.wait_recv()
            pseudo = g[...] - (l[...] + other[...]) * 0.5
            moment = 0.9 * m[...] + pseudo
            nm[...] = moment
            ng[...] = g[...] - 0.7 * (pseudo + 0.9 * moment)
            for a, b, s in ((ng, ng_hbm, 0), (nm, nm_hbm, 1)):
                copy = pltpu.make_async_copy(a, b, out_sem.at[s])
                copy.start()
                outs.append(copy)
        elif kind == "mm":
            offset = PLANES[event[1]]
            z = shifted("z", offset)
            width = xs.shape[1] // SIZES["z"]
            rows = xs[:, pl.ds(pl.multiple_of(z * width, width), width)]
            part = lax.dot_general(rows, cs[...], (((0,), (0,)), ((), ())), preferred_element_type=jnp.float32)
            pb[z] = part.reshape(pb.shape[1:])
            copy = remote(pb.at[z, :, :, 1 - me_c], pp.at[z], pp_s.at[event[1]], pp_r.at[event[1]], core)
            copy.start()
            plane_copies[offset] = copy
        elif kind == "go":
            _, q, sign = event
            d = RS_ORDERS[q][0]
            if d == "z":
                plane_wait((sign * dict(arms(SIZES[d], q % 2))[sign]) % SIZES[d])
            else:
                for offset in PLANES:
                    plane_wait(offset)
            rs_send(q, 0, sign, 0)
        elif kind == "rs":
            _, q, k, sign, j = event
            rs_copies[q, k, sign, j].wait_recv()
            d = RS_ORDERS[q][k]
            if k == 0 and d == "z":
                plane_wait((sign * (dict(arms(SIZES[d], q % 2))[sign] - j - 1)) % SIZES[d])
            rs_send(q, k, sign, j + 1)
        elif kind == "fin":
            _, q, k = event
            d = RS_ORDERS[q][k]
            ends = []
            for sign, length in arms(SIZES[d], q % 2):
                rs_copies[q, k, sign, length - 1].wait_recv()
                ends.append(rs_slot[q, k, sign, length - 1])
            if k == 0 and d == "z":
                plane_wait(0)
            for index, first, count in pieces(q, k, at[d]):
                v = own(q, k, index, count)
                for slot in ends:
                    v = v + decode(got[slot + first : slot + first + count])
                if k < 2:
                    spot = pb.at[index["z"], index["x"], index["y"], me_c, :, cols(q)]
                    spot[...] = v.reshape(spot.shape)
                else:
                    vg[:, q * LANES : (q + 1) * LANES] = v.reshape(ROWS, LANES) * factor
            if k < 2:
                for sign, _ in arms(SIZES[RS_ORDERS[q][k + 1]], q % 2):
                    rs_send(q, k + 1, sign, 0)
        elif kind == "ag":
            _, i, k, sign, j = event
            d = AG_CHUNKS[i][2][k]
            ag_copies[i, k, sign, j].wait_recv()
            if j + 1 < dict(arms(SIZES[d], i % 2))[sign]:
                ag_send(i, k, sign, j + 1)
            ag_seen[i, k] = ag_seen.get((i, k), 0) + 1
            if ag_seen[i, k] == SIZES[d] - 1 and k < 2:
                ag_phase(i, k + 1)
            region = ag_region(i, k, sign, j + 1)
            remote(region, region, fw_s, fw_r, core).start()
        elif kind == "tg":
            if not gathered[0]:
                gathered[0] = True
                everything.wait_recv()
            z = event[1]
            width = tg.shape[1] // SIZES["z"]
            part = lax.dot_general(
                cs[...], w[z].reshape(width, w.shape[-1]), (((1,), (1,)), ((), ())), preferred_element_type=jnp.float32
            )
            tg[:, z * width : (z + 1) * width] = part.astype(jnp.bfloat16)
            copy = pltpu.make_async_copy(
                tg.at[:, pl.ds(z * width, width)], tg_hbm.at[:, pl.ds(z * width, width)], out_sem.at[3 + z]
            )
            copy.start()
            outs.append(copy)
    copy = pltpu.make_async_copy(vg, vg_hbm, out_sem.at[2])
    copy.start()
    outs.append(copy)
    for copy in list(ag_copies.values()) + list(rs_copies.values()) + list(plane_copies.values()) + [everything, hop1, hop2]:
        copy.wait_send()
    for copy in outs:
        copy.wait()


def shards(tokens, value_cot, value_weight, global_params, local_params, momentum):
    tok, d = tokens.shape
    kvw = value_cot.shape[1]
    frag = global_params.shape[0]
    flat = (frag // LANES, LANES)
    nz, nx, ny = (SIZES[k] for k in "zxy")
    plan = Plan()
    n_ag = len(AG_CHUNKS) * sum(s - 1 for s in SIZES.values())
    n_rs = len(RS_ORDERS) * sum(s - 1 for s in SIZES.values())
    blocks = len(RS_ORDERS) * (nz * nx * ny - 1)
    f32, bf16 = jnp.float32, jnp.bfloat16
    factor = float((tok * 2 * nz * nx * ny) ** -0.5)
    dma = pltpu.SemaphoreType.DMA
    anywhere = pl.BlockSpec(memory_space=pl.ANY)
    tg, vg, ng, nm = pl.pallas_call(
        functools.partial(kernel, plan, factor),
        out_shape=(
            jax.ShapeDtypeStruct((tok, d), bf16),
            jax.ShapeDtypeStruct((ROWS, kvw), f32),
            jax.ShapeDtypeStruct(flat, f32),
            jax.ShapeDtypeStruct(flat, f32),
        ),
        in_specs=[anywhere] * 6,
        out_specs=(anywhere,) * 4,
        scratch_shapes=[
            pltpu.VMEM((tok, d), bf16),
            pltpu.VMEM((tok, kvw), bf16),
            pltpu.VMEM((nz, nx, ny, 2, ROWS, kvw), bf16),
            pltpu.VMEM((nz, nx, ny, 2, ROWS, kvw), f32),
            pltpu.VMEM((nz, nx, ny, ROWS, kvw), f32),
            pltpu.VMEM((blocks, ROWS, LANES), bf16),
            pltpu.VMEM((blocks, ROWS, LANES), bf16),
            pltpu.VMEM((tok, d), bf16),
            pltpu.VMEM((ROWS, kvw), f32),
        ]
        + [pltpu.VMEM(flat, f32)] * 7
        + [
            dma((6,)),
            dma((3 + nz,)),
            dma((n_ag,)),
            dma((n_ag,)),
            dma,
            dma,
            dma((nz,)),
            dma((nz,)),
            dma((n_rs,)),
            dma((n_rs,)),
            dma((2,)),
            dma((2,)),
        ],
        compiler_params=pltpu.CompilerParams(
            collective_id=0, has_side_effects=True, vmem_limit_bytes=67043328
        ),
        name="step",
    )(
        tokens,
        value_cot,
        value_weight.reshape(ROWS, kvw),
        global_params.reshape(flat),
        local_params.reshape(flat),
        momentum.reshape(flat),
    )
    return tg, vg[None], ng.reshape(frag), nm.reshape(frag)


def solution(mesh):
    n = mesh.shape["fsdp"]
    split = Mesh(mesh.devices.reshape(mesh.shape["rep"], n // 16, 4, 2, 2), AXES)
    return jax.shard_map(
        shards,
        mesh=split,
        in_specs=(
            P(AXES, None),
            P(AXES, None),
            P("rep", FSDP, None),
            P(FSDP),
            P("rep", FSDP),
            P(FSDP),
        ),
        out_specs=(P(AXES, None), P("rep", FSDP, None), P(FSDP), P(FSDP)),
        check_vma=False,
    )
```

time: 406 us -> 92.9 us (0.23)
  waiting for transfers between devices: 341 us -> 0 us
  Pallas kernels: 0 us -> 84.1 us
  blocking collectives: 19.6 us -> 0 us
  matrix products: 16 us -> 0 us
  between operations: 15.5 us -> 0.67 us
  other arithmetic: 5.2 us -> 0 us
    all_gather x1 -> x0, waiting for transfers between devices: 173 us -> none  [shards(): lax.all_gather(weight, FSDP, axis=0, tiled=True)]
    reduce_scatter x2 -> x0, waiting for transfers between devices: 168 us -> none  [the longest x1 135 us: summed_rows(): return lax.psum_scatter(tiles, chips, scatter_dimension=0, tiled=True)[0]]
    pallas_call x0 -> x1, Pallas kernels: none -> 84.1 us  [shards(): pl.pallas_call(functools.partial(kernel, plan, factor), out_shape=(jax.Sh...]
    all_to_all x1 -> x0, blocking collectives: 19.6 us -> none  [copy_for_each(): lax.all_to_all(jnp.broadcast_to(x[None], (length, *x.shape)), axis, 0, 0,...]
    dot_general x2 -> x0, matrix products: 16 us -> none  [the longest x1 9.49 us: shards(): lax.dot_general(value_cot, lax.all_gather(weight, FSDP, axis=0, tiled=Tru...]
    transpose x1 -> x0, local copies, waits for them, and re-layouts: 6.06 us -> none  [summed_rows(): tiles = tiles.reshape(*sizes, *inside).swapaxes(0, 1).reshape(-1, *inside)]
    unnamed x6 -> x10, local copies, waits for them, and re-layouts: 1.19 us -> 7.11 us
  transfers between devices with their start and end apart: 3 -> 0, of which waited for: 3 -> 0; matrix products, arithmetic and copies ran while one was open for 3% -> 0% of each run, Pallas kernels for 0% -> 0%
where the time goes in v1:
time: 92.9 us; the launch traced here: 91.8 us
  Pallas kernels  84.1 us (91%)
  local copies, waits for them, and re-layouts  7.11 us (8%)
    pallas_call x1, Pallas kernels, shards(): pl.pallas_call(functools.partial(kernel, plan, factor), out_shape=(jax.Sh...  84.1 us
    unnamed x10, local copies, waits for them, and re-layouts  7.11 us

profile of v1, /device:TPU:16, one launch (start us, length us, event | category | flops | bytes accessed | tf_op | source)
XLA Modules:
  0.0 91.8 jit_solution(17477333707847291238)
XLA Ops:
  0.6 84.1 %step.1 = (bf16[512,4096]{1,0:T(8,128)(2,1)}, f32[32,1024]{1,0:T(8,128)}, f32[1024,128]{1,0:T(8,128)}, f32[1024,128]{1,0:T(8,128)}) custom-call(bf16[512,4096]{1,0:T(8,128)(2,1)} %x_hbm.1, bf16[512,1024]{1,0:T(8,128)(2,1)} %cot_hbm.1, bf16[32,1024]{1,0:T(8,128)(2,1)} %bitcast.13, f32[1024,128]{1,0:T(8,128)} %bitcast.9, f32[1024,128]{1,0:T(8,128)} %bitcast.10, ...), custom_call_target="tpu_custom_call" | custom-call | tf_op jit(solution)/shard_map/step/pallas_call | solution.py:433
  84.7 0.0 copy-start.2
  84.7 0.0 copy-start.1
  84.7 0.0 copy-start
  84.7 4.8 %copy.14 = bf16[512,4096]{1,0:T(8,128)(2,1)} copy(bf16[512,4096]{1,0:T(8,128)(2,1)} %get-tuple-element.16) | data formatting | bytes 8388608
  89.5 0.0 copy-done.2
  89.5 0.7 copy.15
  90.2 0.0 copy-done.1
  90.2 0.8 copy.16
  91.0 0.0 copy-done
  91.0 0.8 copy.17
Async XLA Ops:
  84.7 4.8 %copy-start.2 = (f32[32,1024]{1,0:T(8,128)S(1)}, f32[32,1024]{1,0:T(8,128)}, u32[]{:S(2)}) copy-start(f32[32,1024]{1,0:T(8,128)} %get-tuple-element.9) | copy-start | bytes 393220
  84.7 5.5 %copy-start.1 = (f32[1024,128]{1,0:T(8,128)S(1)}, f32[1024,128]{1,0:T(8,128)}, u32[]{:S(2)}) copy-start(f32[1024,128]{1,0:T(8,128)} %get-tuple-element.10) | copy-start | bytes 1572868
  84.7 6.3 %copy-start = (f32[1024,128]{1,0:T(8,128)S(1)}, f32[1024,128]{1,0:T(8,128)}, u32[]{:S(2)}) copy-start(f32[1024,128]{1,0:T(8,128)} %get-tuple-element.11) | copy-start | bytes 1572868

commit v2 on v1

v2 whole, which is shorter than its diff:
```python
import functools

import jax
import jax.numpy as jnp
from jax import lax
from jax.experimental import pallas as pl
from jax.experimental.pallas import tpu as pltpu
from jax.sharding import Mesh
from jax.sharding import PartitionSpec as P

MESH_ID = pl.DeviceIdType.MESH
AXES = ("rep", "z", "x", "y", "c")
FSDP = AXES[1:]
SIZES = {"z": 8, "x": 4, "y": 2}
ROWS = 32
LANES = 128

RS = (("zxy", 0, 0), ("xyz", 1, 0), ("xyz", 0, 0), ("zxy", 1, 1), ("yxz", 0, 1), ("xyz", 1, 1), ("xyz", 0, 1), ("yzx", 0, 1))
AG = ((0, 1, "xzy", 1, 1), (1, 1, "yxz", 1, 3), (2, 1, "yzx", 1, 1), (3, 1, "xyz", 0, 1), (4, 1, "xzy", 1, 0), (5, 1, "yzx", 1, 3), (6, 1, "xyz", 0, 4), (7, 1, "zyx", 0, 4))
PAIRS = (0, 1, 2, 3)

SCALE = 2.0**-3
LOW = 2.0**-4
HIGH = 2.0**10


def encode(v):
    u = v * SCALE
    a = jnp.abs(u)
    p = a * jnp.clip(a, LOW, HIGH)
    p = p * p
    p = p * p
    return jnp.where(u < 0, -p, p).astype(jnp.bfloat16)


def decode(coded):
    y = coded.astype(jnp.float32)
    a = jnp.abs(y)
    r = lax.rsqrt(lax.rsqrt(a))
    m = r * lax.rsqrt(r)
    end = r * jnp.where(a < 1.0, 1.0 / (LOW * SCALE), 1.0 / (HIGH * SCALE))
    v = jnp.where((a < LOW**8) | (a > HIGH**8), end, m * (1.0 / SCALE))
    return jnp.where(y < 0, -v, v)


def arms(n, flip):
    if n == 2:
        return ((1, 1),)
    long, short = n // 2, n - 1 - n // 2
    return ((1, long), (-1, short)) if flip else ((1, short), (-1, long))


def far_first(n):
    return sorted((i if 2 * i <= n else i - n for i in range(1, n)), key=lambda i: (-abs(i), i))


def link(dim, sign):
    return dim if SIZES[dim] == 2 else dim + ("+" if sign > 0 else "-")


class Plan:
    RATE = 44e3
    HOP = 2.4

    def __init__(self, rs=RS, ag=AG, pairs=PAIRS):
        self.rs, self.ag, self.pairs = rs, ag, pairs
        self.order = []
        self.tc = 0.0
        self.links = {}
        self.ready = []
        self.serial = 0
        self.last = {}
        self.held = []
        self.pairs_done = 0
        self.run()

    def send(self, name, size, rate=None, hop=None):
        begin = max(self.links.get(name, 0.0), self.tc)
        self.links[name] = begin + size / (rate or self.RATE)
        return self.links[name] + (hop or self.HOP)

    def add(self, time, priority, event, duration):
        self.ready.append((time, priority, self.serial, event, duration))
        self.serial += 1

    def rs_arms(self, q, k):
        order, flip, straight = self.rs[q]
        n = SIZES[order[k]]
        if k == 2 and straight:
            return tuple((by, 1) for by in far_first(n))
        return arms(n, flip)

    def ag_arms(self, i, k):
        return arms(SIZES[self.ag[i][2][k]], self.ag[i][3])

    def nb(self, q, k):
        n = 1
        for d in self.rs[q][0][k + 1 :]:
            n *= SIZES[d]
        return n

    def rs_send(self, q, k, sign, j):
        nb = self.nb(q, k)
        at = self.send(link(self.rs[q][0][k], sign), abs(sign) * nb * ROWS * LANES * 2)
        at += 0.75 * (abs(sign) - 1)
        if j + 1 < dict(self.rs_arms(q, k))[sign]:
            self.add(at, 0, ("rs", q, k, sign, j), 0.1 + 0.02 * nb)
        else:
            got = self.last.setdefault((q, k), {})
            got[sign] = at
            if len(got) == len(self.rs_arms(q, k)):
                self.add(max(got.values()), 0, ("fin", q, k), 0.15 + 0.05 * nb)

    def ag_bytes(self, i, k):
        n = ROWS * LANES * self.ag[i][1] * 2
        for d in self.ag[i][2][:k]:
            n *= SIZES[d]
        return n

    def ag_send(self, i, k, sign, j):
        at = self.send(link(self.ag[i][2][k], sign), self.ag_bytes(i, k))
        self.add(at, 0, ("ag", i, k, sign, j), 0.05)

    def ag_phase(self, i, k):
        for sign, _ in self.ag_arms(i, k):
            self.ag_send(i, k, sign, 0)

    def release(self):
        for i, k in list(self.held):
            if k < 2 or self.ag[i][4] <= self.pairs_done:
                self.held.remove((i, k))
                self.add(self.tc, 0.5, ("agp", i, k), 0.05)

    def run(self):
        seen = {}
        planes = SIZES["z"]
        pieces = len(self.ag) * sum(n - 1 for n in SIZES.values())
        self.tc = 2.0
        self.add(2.0, 0, ("start",), 0.5)
        for z in range(planes):
            self.add(3.0, 1, ("xt", z), 0.2)
        while self.ready:
            now = [r for r in self.ready if r[0] <= self.tc]
            pick = min(now, key=lambda r: (r[1], r[0], r[2])) if now else min(self.ready)
            self.ready.remove(pick)
            event = pick[3]
            self.tc = max(self.tc, pick[0]) + pick[4]
            self.order.append(event)
            kind = event[0]
            if kind == "start":
                for i in range(len(self.ag)):
                    self.ag_phase(i, 0)
                self.add(self.send("y", 524288), 1, ("relay",), 0.1)
            elif kind == "relay":
                self.add(self.send("cross", 524288), 2, ("outer",), 0.6)
            elif kind == "xt":
                at = self.send("core", 1 << 18, 5e5, 1.0)
                seen["xt"] = seen.get("xt", 0) + 1
                if seen["xt"] == planes:
                    for n, pair in enumerate(self.pairs):
                        self.add(at, 1 + 0.1 * n, ("mm", pair), 0.9)
            elif kind == "mm":
                for q in (2 * event[1], 2 * event[1] + 1):
                    for sign, _ in self.rs_arms(q, 0):
                        self.add(self.tc, 0, ("go", q, sign), 0.1 + 0.02 * self.nb(q, 0))
                self.pairs_done += 1
                self.release()
            elif kind == "agp":
                self.ag_phase(event[1], event[2])
            elif kind == "go":
                self.rs_send(event[1], 0, event[2], 0)
            elif kind == "rs":
                self.rs_send(event[1], event[2], event[3], event[4] + 1)
            elif kind == "fin":
                _, q, k = event
                if k < 2:
                    for sign, _ in self.rs_arms(q, k + 1):
                        self.rs_send(q, k + 1, sign, 0)
            elif kind == "ag":
                _, i, k, sign, j = event
                self.send("core", self.ag_bytes(i, k), 5e5, 1.0)
                if j + 1 < dict(self.ag_arms(i, k))[sign]:
                    self.ag_send(i, k, sign, j + 1)
                seen[i, k] = seen.get((i, k), 0) + 1
                pieces -= 1
                if seen[i, k] == SIZES[self.ag[i][2][k]] - 1 and k < 2:
                    self.held.append((i, k + 1))
                    self.release()
                if not pieces:
                    for z in range(planes):
                        self.add(self.tc + 3.0, 3, ("tg", z), 0.6)


def kernel(plan, factor, x_hbm, cot_hbm, w_hbm, g_hbm, l_hbm, m_hbm, tg, vg, ng, nm,
           xs, cs, xt, px, pc, w, pb, got, put, g, l, m, mid, other,
           in_sem, ag_s, ag_r, fw_s, fw_r, sw_s, sw_r, rs_s, rs_r, rep_s, rep_r):
    at = {name: lax.axis_index(name) for name in AXES}
    me_c = at["c"]

    def peer(**moved):
        return tuple(moved.get(name, at[name]) for name in AXES)

    def towards(dim, sign):
        n = SIZES[dim]
        return peer(**{dim: lax.rem(at[dim] + (sign + n), n)})

    def shifted(dim, by):
        n = SIZES[dim]
        return lax.rem(at[dim] + (by % n), n)

    core = peer(c=1 - me_c)
    across = peer(rep=1 - at["rep"], y=1 - at["y"])
    peers = [core, across]
    for dim in SIZES:
        peers += [towards(dim, sign) for sign, _ in arms(SIZES[dim], 0)]

    local = [
        pltpu.make_async_copy(w_hbm, w.at[at["z"], at["x"], at["y"], me_c], in_sem.at[0]),
        pltpu.make_async_copy(cot_hbm, cs, in_sem.at[1]),
        pltpu.make_async_copy(l_hbm, l, in_sem.at[3]),
        pltpu.make_async_copy(x_hbm, xs, in_sem.at[2]),
        pltpu.make_async_copy(g_hbm, g, in_sem.at[4]),
        pltpu.make_async_copy(m_hbm, m, in_sem.at[5]),
    ]
    for copy in local:
        copy.start()
    barrier = pltpu.get_barrier_semaphore()
    for device in peers:
        pl.semaphore_signal(barrier, inc=1, device_id=device, device_id_type=MESH_ID)
    pl.semaphore_wait(barrier, len(peers))

    def remote(src, dst, send, recv, device):
        return pltpu.make_async_remote_copy(
            src_ref=src, dst_ref=dst, send_sem=send, recv_sem=recv, device_id=device, device_id_type=MESH_ID
        )

    ag_copies, rs_copies, rs_slot = {}, {}, {}
    used = {"ag": 0, "rs": 0, "block": 0}

    def ag_region(i, k, sign, j):
        tile, tiles, order = plan.ag[i][:3]
        index = {d: slice(None) for d in order[:k]}
        index[order[k]] = shifted(order[k], -sign * j)
        for d in order[k + 1 :]:
            index[d] = at[d]
        return w.at[index["z"], index["x"], index["y"], me_c, :, pl.ds(tile * LANES, tiles * LANES)]

    def ag_send(i, k, sign, j):
        n = used["ag"]
        used["ag"] += 1
        region = ag_region(i, k, sign, j)
        copy = remote(region, region, ag_s.at[n], ag_r.at[n], towards(plan.ag[i][2][k], sign))
        copy.start()
        ag_copies[i, k, sign, j] = copy

    def ag_phase(i, k):
        for sign, _ in plan.ag_arms(i, k):
            ag_send(i, k, sign, 0)

    def pieces(q, k, dest):
        order = plan.rs[q][0]
        index = {d: at[d] for d in order[:k]}
        index[order[k]] = dest
        free = sorted(order[k + 1 :], key="zxy".index)
        if not free:
            yield dict(index), 0, 1
        elif len(free) == 1 and SIZES[free[0]] <= 4:
            n = SIZES[free[0]]
            yield {**index, free[0]: slice(None)}, 0, n
        elif len(free) == 1:
            n = SIZES[free[0]]
            for h in range(n // 4):
                yield {**index, free[0]: pl.ds(4 * h, 4)}, 4 * h, 4
        else:
            inner = SIZES[free[1]]
            for o in range(SIZES[free[0]]):
                yield {**index, free[0]: o, free[1]: slice(None)}, o * inner, inner

    def cols(q):
        return pl.ds(q * LANES, LANES)

    def own(q, index, n):
        return pb[index["z"], index["x"], index["y"], :, cols(q)].reshape(n, ROWS, LANES)

    def rs_send(q, k, sign, j):
        d = plan.rs[q][0][k]
        length = dict(plan.rs_arms(q, k))[sign]
        nb = plan.nb(q, k)
        base = used["block"]
        used["block"] += nb
        n = used["rs"]
        used["rs"] += 1
        before = rs_slot.get((q, k, sign, j - 1))
        for index, first, count in pieces(q, k, shifted(d, sign * (length - j))):
            v = own(q, index, count)
            if before is not None:
                v = v + decode(got[before + first : before + first + count])
            put[base + first : base + first + count] = encode(v)
        copy = remote(put.at[pl.ds(base, nb)], got.at[pl.ds(base, nb)], rs_s.at[n], rs_r.at[n], towards(d, sign))
        copy.start()
        rs_copies[q, k, sign, j] = copy
        rs_slot[q, k, sign, j] = base

    swaps = []
    done = set()
    forwarded = w.at[:, :, :, me_c]
    everything = remote(forwarded, forwarded, fw_s, fw_r, core)
    hop1 = remote(l, mid, rep_s.at[0], rep_r.at[0], towards("y", 1))
    hop2 = remote(mid, other, rep_s.at[1], rep_r.at[1], across)
    planes = SIZES["z"]
    width = xs.shape[1] // planes

    for event in plan.order:
        kind = event[0]
        if kind == "start":
            local[0].wait()
            for i in range(len(plan.ag)):
                ag_phase(i, 0)
            mine = w.at[at["z"], at["x"], at["y"], me_c]
            remote(mine, mine, fw_s, fw_r, core).start()
            local[1].wait()
            copy = remote(cs, pc, sw_s.at[planes], sw_r.at[planes], core)
            copy.start()
            swaps.append(copy)
            local[2].wait()
            hop1.start()
            local[3].wait()
        elif kind == "relay":
            hop1.wait_recv()
            hop2.start()
        elif kind == "outer":
            local[4].wait()
            local[5].wait()
            hop2.wait_recv()
            pseudo = g[...] - (l[...] + other[...]) * 0.5
            moment = 0.9 * m[...] + pseudo
            nm[...] = moment
            ng[...] = g[...] - 0.7 * (pseudo + 0.9 * moment)
        elif kind == "xt":
            z = event[1]
            xt[z] = xs[:, z * width : (z + 1) * width].T.reshape(xt.shape[1:])
            copy = remote(xt.at[z, :, :, 1 - me_c], px.at[z], sw_s.at[z], sw_r.at[z], core)
            copy.start()
            swaps.append(copy)
        elif kind == "mm":
            if kind not in done:
                done.add(kind)
                for copy in swaps:
                    copy.wait_recv()
            two = pl.ds(event[1] * 2 * LANES, 2 * LANES)
            half = planes // 2
            for h in (0, half):
                rows = xt[h : h + half, :, :, me_c].reshape(-1, xt.shape[-1])
                more = px[h : h + half].reshape(-1, px.shape[-1])
                part = jnp.dot(rows, cs[:, two], preferred_element_type=jnp.float32)
                part = part + jnp.dot(more, pc[:, two], preferred_element_type=jnp.float32)
                pb[h : h + half, :, :, :, two] = part.reshape((half,) + pb.shape[1:4] + (2 * LANES,))
        elif kind == "agp":
            ag_phase(event[1], event[2])
        elif kind == "go":
            rs_send(event[1], 0, event[2], 0)
        elif kind == "rs":
            _, q, k, sign, j = event
            rs_copies[q, k, sign, j].wait_recv()
            rs_send(q, k, sign, j + 1)
        elif kind == "fin":
            _, q, k = event
            ends = []
            for sign, length in plan.rs_arms(q, k):
                rs_copies[q, k, sign, length - 1].wait_recv()
                ends.append(rs_slot[q, k, sign, length - 1])
            for index, first, count in pieces(q, k, at[plan.rs[q][0][k]]):
                v = own(q, index, count)
                for slot in ends:
                    v = v + decode(got[slot + first : slot + first + count])
                if k < 2:
                    spot = pb.at[index["z"], index["x"], index["y"], :, cols(q)]
                    spot[...] = v.reshape(spot.shape)
                else:
                    vg[:, q * LANES : (q + 1) * LANES] = v.reshape(ROWS, LANES) * factor
            if k < 2:
                for sign, _ in plan.rs_arms(q, k + 1):
                    rs_send(q, k + 1, sign, 0)
        elif kind == "ag":
            _, i, k, sign, j = event
            ag_copies[i, k, sign, j].wait_recv()
            if j + 1 < dict(plan.ag_arms(i, k))[sign]:
                ag_send(i, k, sign, j + 1)
            region = ag_region(i, k, sign, j + 1)
            remote(region, region, fw_s, fw_r, core).start()
        elif kind == "tg":
            if kind not in done:
                done.add(kind)
                everything.wait_recv()
            z = event[1]
            part = lax.dot_general(
                cs[...], w[z].reshape(width, w.shape[-1]), (((1,), (1,)), ((), ())), preferred_element_type=jnp.float32
            )
            tg[:, z * width : (z + 1) * width] = part.astype(jnp.bfloat16)
    for copy in [*ag_copies.values(), *rs_copies.values(), *swaps, everything, hop1, hop2]:
        copy.wait_send()


def finish(*refs):
    n = len(refs) // 2
    sem = refs[-1]
    copies = [pltpu.make_async_copy(refs[i], refs[n + i], sem.at[i]) for i in range(n)]
    for copy in copies:
        copy.start()
    for copy in copies:
        copy.wait()


def shards(tokens, value_cot, value_weight, global_params, local_params, momentum):
    tok, d = tokens.shape
    kvw = value_cot.shape[1]
    frag = global_params.shape[0]
    flat = (frag // LANES, LANES)
    nz, nx, ny = (SIZES[k] for k in "zxy")
    plan = Plan()
    n_ag = len(plan.ag) * sum(s - 1 for s in SIZES.values())
    n_rs = len(plan.rs) * sum(s - 1 for s in SIZES.values())
    blocks = len(plan.rs) * (nz * nx * ny - 1)
    f32, bf16 = jnp.float32, jnp.bfloat16
    factor = float((tok * 2 * nz * nx * ny) ** -0.5)
    dma = pltpu.SemaphoreType.DMA
    anywhere = pl.BlockSpec(memory_space=pl.ANY)
    tg, vg, ng, nm = pl.pallas_call(
        functools.partial(kernel, plan, factor),
        out_shape=(
            pltpu.VMEM((tok, d), bf16),
            pltpu.VMEM((ROWS, kvw), f32),
            pltpu.VMEM(flat, f32),
            pltpu.VMEM(flat, f32),
        ),
        in_specs=[anywhere] * 6,
        out_specs=(pl.BlockSpec(memory_space=pltpu.VMEM),) * 4,
        scratch_shapes=[
            pltpu.VMEM((tok, d), bf16),
            pltpu.VMEM((tok, kvw), bf16),
            pltpu.VMEM((nz, nx, ny, 2, ROWS, tok), bf16),
            pltpu.VMEM((nz, nx, ny, ROWS, tok), bf16),
            pltpu.VMEM((tok, kvw), bf16),
            pltpu.VMEM((nz, nx, ny, 2, ROWS, kvw), bf16),
            pltpu.VMEM((nz, nx, ny, ROWS, kvw), f32),
            pltpu.VMEM((blocks, ROWS, LANES), bf16),
            pltpu.VMEM((blocks, ROWS, LANES), bf16),
        ]
        + [pltpu.VMEM(flat, f32)] * 5
        + [
            dma((6,)),
            dma((n_ag,)),
            dma((n_ag,)),
            dma,
            dma,
            dma((nz + 1,)),
            dma((nz + 1,)),
            dma((n_rs,)),
            dma((n_rs,)),
            dma((2,)),
            dma((2,)),
        ],
        compiler_params=pltpu.CompilerParams(
            collective_id=0, has_side_effects=True, vmem_limit_bytes=58 * 2**20
        ),
        name="step",
    )(
        tokens,
        value_cot,
        value_weight.reshape(ROWS, kvw),
        global_params.reshape(flat),
        local_params.reshape(flat),
        momentum.reshape(flat),
    )
    outs = (tg, vg, ng, nm)
    tg, vg, ng, nm = pl.pallas_call(
        finish,
        out_shape=tuple(jax.ShapeDtypeStruct(o.shape, o.dtype) for o in outs),
        in_specs=[anywhere] * len(outs),
        out_specs=(anywhere,) * len(outs),
        scratch_shapes=[dma((len(outs),))],
        compiler_params=pltpu.CompilerParams(vmem_limit_bytes=2**20),
        name="finish",
    )(*outs)
    return tg, vg[None], ng.reshape(frag), nm.reshape(frag)


def solution(mesh):
    n = mesh.shape["fsdp"]
    split = Mesh(mesh.devices.reshape(mesh.shape["rep"], n // 16, 4, 2, 2), AXES)
    return jax.shard_map(
        shards,
        mesh=split,
        in_specs=(
            P(AXES, None),
            P(AXES, None),
            P("rep", FSDP, None),
            P(FSDP),
            P("rep", FSDP),
            P(FSDP),
        ),
        out_specs=(P(AXES, None), P("rep", FSDP, None), P(FSDP), P(FSDP)),
        check_vma=False,
    )
```

time: 92.9 us -> 67.5 us (0.73)
  Pallas kernels: 84.1 us -> 66 us
  local copies, waits for them, and re-layouts: 7.11 us -> 0 us
    pallas_call x1 -> x2, Pallas kernels: 84.1 us -> 66 us  [the longest x1 63.6 us: shards(): pl.pallas_call(functools.partial(kernel, plan, factor), out_shape=(pltpu....]
    unnamed x10 -> x0, local copies, waits for them, and re-layouts: 7.11 us -> none
where the time goes in v2:
time: 67.5 us; the launch traced here: 66.8 us
  Pallas kernels  66 us (98%)
  between operations  0.8 us (1%)
    pallas_call x1, Pallas kernels, shards(): pl.pallas_call(functools.partial(kernel, plan, factor), out_shape=(pltpu....  63.6 us
    pallas_call x1, Pallas kernels, shards(): pl.pallas_call(finish, out_shape=tuple((jax.ShapeDtypeStruct(o.shape, o.d...  2.41 us

profile of v2, /device:TPU:16, one launch (start us, length us, event | category | flops | bytes accessed | tf_op | source)
XLA Modules:
  0.0 66.8 jit_solution(16337756148487042081)
XLA Ops:
  0.6 63.6 %step.1 = (bf16[512,4096]{1,0:T(8,128)(2,1)S(1)}, f32[32,1024]{1,0:T(8,128)S(1)}, f32[1024,128]{1,0:T(8,128)S(1)}, f32[1024,128]{1,0:T(8,128)S(1)}) custom-call(bf16[512,4096]{1,0:T(8,128)(2,1)} %x_hbm.1, bf16[512,1024]{1,0:T(8,128)(2,1)} %cot_hbm.1, bf16[32,1024]{1,0:T(8,128)(2,1)} %bitcast.10, f32[1024,128]{1,0:T(8,128)} %bitcast.7, f32[1024,128]{1,0:T(8,128)} %bitcast.8, ...), custom_call_target="tpu_custom_call" | custom-call | tf_op jit(solution)/shard_map/step/pallas_call | solution.py:428
  64.2 2.4 %finish.1 = (bf16[512,4096]{1,0:T(8,128)(2,1)}, f32[32,1024]{1,0:T(8,128)}, f32[1024,128]{1,0:T(8,128)}, f32[1024,128]{1,0:T(8,128)}) custom-call(bf16[512,4096]{1,0:T(8,128)(2,1)S(1)} %get-tuple-element.12.refs_0_, f32[32,1024]{1,0:T(8,128)S(1)} %get-tuple-element.13.refs_1_, f32[1024,128]{1,0:T(8,128)S(1)} %get-tuple-element.14.refs_2_, ...), custom_call_target="tpu_custom_call" | custom-call | tf_op jit(solution)/shard_map/finish/pallas_call | solution.py:476

commit v3 on v2

--- a/solution.py
+++ b/solution.py
@@ -15,9 +15,12 @@
 ROWS = 32
 LANES = 128
 
-RS = (("zxy", 0, 0), ("xyz", 1, 0), ("xyz", 0, 0), ("zxy", 1, 1), ("yxz", 0, 1), ("xyz", 1, 1), ("xyz", 0, 1), ("yzx", 0, 1))
-AG = ((0, 1, "xzy", 1, 1), (1, 1, "yxz", 1, 3), (2, 1, "yzx", 1, 1), (3, 1, "xyz", 0, 1), (4, 1, "xzy", 1, 0), (5, 1, "yzx", 1, 3), (6, 1, "xyz", 0, 4), (7, 1, "zyx", 0, 4))
+RS = (("xyz", 1, 0), ("yzx", 1, 1), ("zyx", 1, 1), ("xzy", 0, 1), ("yzx", 0, 1), ("xzy", 0, 0), ("xzy", 0, 0), ("yzx", 0, 1))
+AG = ((0, 1, "yzx", 1, 2), (1, 1, "xzy", 0, 1), (2, 2, "yxz", 1, 1), (4, 1, "xzy", 0, 4), (5, 1, "yzx", 0, 2), (6, 2, "yzx", 1, 0))
+PARTS = 2
+TILES = 8
 PAIRS = (0, 1, 2, 3)
+REP = (2.0, 2.0, 2.0, 24.0)
 
 SCALE = 2.0**-3
 LOW = 2.0**-4
@@ -62,8 +65,8 @@
     RATE = 44e3
     HOP = 2.4
 
-    def __init__(self, rs=RS, ag=AG, pairs=PAIRS):
-        self.rs, self.ag, self.pairs = rs, ag, pairs
+    def __init__(self, rs=RS, ag=AG, pairs=PAIRS, rep=REP):
+        self.rs, self.ag, self.pairs, self.rep = rs, ag, pairs, rep
         self.order = []
         self.tc = 0.0
         self.links = {}
@@ -72,6 +75,7 @@
         self.last = {}
         self.held = []
         self.pairs_done = 0
+        self.parts_done = 0
         self.run()
 
     def send(self, name, size, rate=None, hop=None):
@@ -82,6 +86,9 @@
     def add(self, time, priority, event, duration):
         self.ready.append((time, priority, self.serial, event, duration))
         self.serial += 1
+
+    def part(self, i):
+        return self.ag[i][0] * PARTS // TILES
 
     def rs_arms(self, q, k):
         order, flip, straight = self.rs[q]
@@ -134,7 +141,9 @@
     def run(self):
         seen = {}
         planes = SIZES["z"]
-        pieces = len(self.ag) * sum(n - 1 for n in SIZES.values())
+        pieces = [0] * PARTS
+        for i in range(len(self.ag)):
+            pieces[self.part(i)] += sum(n - 1 for n in SIZES.values())
         self.tc = 2.0
         self.add(2.0, 0, ("start",), 0.5)
         for z in range(planes):
@@ -150,9 +159,12 @@
             if kind == "start":
                 for i in range(len(self.ag)):
                     self.ag_phase(i, 0)
-                self.add(self.send("y", 524288), 1, ("relay",), 0.1)
+                for n, time in enumerate(self.rep):
+                    self.add(max(time, self.tc), 0.2, ("rep", n), 0.05)
+            elif kind == "rep":
+                self.add(self.send("y", 524288 // len(self.rep)), 1, ("relay", event[1]), 0.05)
             elif kind == "relay":
-                self.add(self.send("cross", 524288), 2, ("outer",), 0.6)
+                self.add(self.send("cross", 524288 // len(self.rep)), 2, ("outer", event[1]), 0.15)
             elif kind == "xt":
                 at = self.send("core", 1 << 18, 5e5, 1.0)
                 seen["xt"] = seen.get("xt", 0) + 1
@@ -182,17 +194,19 @@
                 if j + 1 < dict(self.ag_arms(i, k))[sign]:
                     self.ag_send(i, k, sign, j + 1)
                 seen[i, k] = seen.get((i, k), 0) + 1
-                pieces -= 1
+                g = self.part(i)
+                pieces[g] -= 1
                 if seen[i, k] == SIZES[self.ag[i][2][k]] - 1 and k < 2:
                     self.held.append((i, k + 1))
                     self.release()
-                if not pieces:
+                if not pieces[g]:
+                    self.parts_done += 1
                     for z in range(planes):
-                        self.add(self.tc + 3.0, 3, ("tg", z), 0.6)
+                        self.add(self.tc + 2.0, 2 + self.parts_done, ("tg", g, z, self.parts_done), 0.1 + 0.5 / PARTS)
 
 
 def kernel(plan, factor, x_hbm, cot_hbm, w_hbm, g_hbm, l_hbm, m_hbm, tg, vg, ng, nm,
-           xs, cs, xt, px, pc, w, pb, got, put, g, l, m, mid, other,
+           xs, cs, xt, px, pc, w, pb, got, put, g, l, m, mid, other, sums,
            in_sem, ag_s, ag_r, fw_s, fw_r, sw_s, sw_r, rs_s, rs_r, rep_s, rep_r):
     at = {name: lax.axis_index(name) for name in AXES}
     me_c = at["c"]
@@ -303,10 +317,21 @@
 
     swaps = []
     done = set()
-    forwarded = w.at[:, :, :, me_c]
-    everything = remote(forwarded, forwarded, fw_s, fw_r, core)
-    hop1 = remote(l, mid, rep_s.at[0], rep_r.at[0], towards("y", 1))
-    hop2 = remote(mid, other, rep_s.at[1], rep_r.at[1], across)
+
+    def in_part(n):
+        return pl.ds(n * TILES // PARTS * LANES, TILES // PARTS * LANES)
+
+    whole = []
+    for n in range(PARTS):
+        forwarded = w.at[:, :, :, me_c, :, in_part(n)]
+        whole.append(remote(forwarded, forwarded, fw_s.at[n], fw_r.at[n], core))
+    n_rep = len(plan.rep)
+    share = l.shape[0] // n_rep
+    hop1, hop2 = [], []
+    for n in range(n_rep):
+        rows = pl.ds(n * share, share)
+        hop1.append(remote(l.at[rows], mid.at[rows], rep_s.at[n], rep_r.at[n], towards("y", 1)))
+        hop2.append(remote(mid.at[rows], other.at[rows], rep_s.at[n_rep + n], rep_r.at[n_rep + n], across))
     planes = SIZES["z"]
     width = xs.shape[1] // planes
 
@@ -317,25 +342,31 @@
             for i in range(len(plan.ag)):
                 ag_phase(i, 0)
             mine = w.at[at["z"], at["x"], at["y"], me_c]
-            remote(mine, mine, fw_s, fw_r, core).start()
+            for n in range(PARTS):
+                part = mine.at[:, in_part(n)]
+                remote(part, part, fw_s.at[n], fw_r.at[n], core).start()
             local[1].wait()
             copy = remote(cs, pc, sw_s.at[planes], sw_r.at[planes], core)
             copy.start()
             swaps.append(copy)
             local[2].wait()
-            hop1.start()
             local[3].wait()
+        elif kind == "rep":
+            hop1[event[1]].start()
         elif kind == "relay":
-            hop1.wait_recv()
-            hop2.start()
+            hop1[event[1]].wait_recv()
+            hop2[event[1]].start()
         elif kind == "outer":
-            local[4].wait()
-            local[5].wait()
-            hop2.wait_recv()
-            pseudo = g[...] - (l[...] + other[...]) * 0.5
-            moment = 0.9 * m[...] + pseudo
-            nm[...] = moment
-            ng[...] = g[...] - 0.7 * (pseudo + 0.9 * moment)
+            if kind not in done:
+                done.add(kind)
+                local[4].wait()
+                local[5].wait()
+            hop2[event[1]].wait_recv()
+            rows = pl.ds(event[1] * share, share)
+            pseudo = g[rows] - (l[rows] + other[rows]) * 0.5
+            moment = 0.9 * m[rows] + pseudo
+            nm[rows] = moment
+            ng[rows] = g[rows] - 0.7 * (pseudo + 0.9 * moment)
         elif kind == "xt":
             z = event[1]
             xt[z] = xs[:, z * width : (z + 1) * width].T.reshape(xt.shape[1:])
@@ -387,17 +418,27 @@
             if j + 1 < dict(plan.ag_arms(i, k))[sign]:
                 ag_send(i, k, sign, j + 1)
             region = ag_region(i, k, sign, j + 1)
-            remote(region, region, fw_s, fw_r, core).start()
+            n = plan.part(i)
+            remote(region, region, fw_s.at[n], fw_r.at[n], core).start()
         elif kind == "tg":
-            if kind not in done:
-                done.add(kind)
-                everything.wait_recv()
-            z = event[1]
+            _, n, z, turn = event
+            if (kind, n) not in done:
+                done.add((kind, n))
+                whole[n].wait_recv()
+            depth = in_part(n)
             part = lax.dot_general(
-                cs[...], w[z].reshape(width, w.shape[-1]), (((1,), (1,)), ((), ())), preferred_element_type=jnp.float32
+                cs[:, depth],
+                w[z, :, :, :, :, depth].reshape(width, -1),
+                (((1,), (1,)), ((), ())),
+                preferred_element_type=jnp.float32,
             )
-            tg[:, z * width : (z + 1) * width] = part.astype(jnp.bfloat16)
-    for copy in [*ag_copies.values(), *rs_copies.values(), *swaps, everything, hop1, hop2]:
+            if turn > 1:
+                part = part + sums[z]
+            if turn < PARTS:
+                sums[z] = part
+            else:
+                tg[:, z * width : (z + 1) * width] = part.astype(jnp.bfloat16)
+    for copy in [*ag_copies.values(), *rs_copies.values(), *swaps, *whole, *hop1, *hop2]:
         copy.wait_send()
 
 
@@ -447,18 +488,19 @@
             pltpu.VMEM((blocks, ROWS, LANES), bf16),
         ]
         + [pltpu.VMEM(flat, f32)] * 5
+        + [pltpu.VMEM((nz, tok, d // nz), f32)]
         + [
             dma((6,)),
             dma((n_ag,)),
             dma((n_ag,)),
-            dma,
-            dma,
+            dma((PARTS,)),
+            dma((PARTS,)),
             dma((nz + 1,)),
             dma((nz + 1,)),
             dma((n_rs,)),
             dma((n_rs,)),
-            dma((2,)),
-            dma((2,)),
+            dma((2 * len(plan.rep),)),
+            dma((2 * len(plan.rep),)),
         ],
         compiler_params=pltpu.CompilerParams(
             collective_id=0, has_side_effects=True, vmem_limit_bytes=58 * 2**20

time: 67.5 us -> 66.5 us (0.985)
  Pallas kernels: 66 us -> 64.8 us
    pallas_call x1, Pallas kernels: 63.6 us -> 62.4 us  [shards(): pl.pallas_call(functools.partial(kernel, plan, factor), out_shape=(pltpu....]
where the time goes in v3:
time: 66.5 us; the launch traced here: 65.6 us
  Pallas kernels  64.8 us (97%)
  between operations  0.8 us (1%)
    pallas_call x1, Pallas kernels, shards(): pl.pallas_call(functools.partial(kernel, plan, factor), out_shape=(pltpu....  62.4 us
    pallas_call x1, Pallas kernels, shards(): pl.pallas_call(finish, out_shape=tuple((jax.ShapeDtypeStruct(o.shape, o.d...  2.41 us

profile of v3, /device:TPU:16, one launch (start us, length us, event | category | flops | bytes accessed | tf_op | source)
XLA Modules:
  0.0 65.6 jit_solution(18113736856554623839)
XLA Ops:
  0.6 62.4 %step.1 = (bf16[512,4096]{1,0:T(8,128)(2,1)S(1)}, f32[32,1024]{1,0:T(8,128)S(1)}, f32[1024,128]{1,0:T(8,128)S(1)}, f32[1024,128]{1,0:T(8,128)S(1)}) custom-call(bf16[512,4096]{1,0:T(8,128)(2,1)} %x_hbm.1, bf16[512,1024]{1,0:T(8,128)(2,1)} %cot_hbm.1, bf16[32,1024]{1,0:T(8,128)(2,1)} %bitcast.10, f32[1024,128]{1,0:T(8,128)} %bitcast.7, f32[1024,128]{1,0:T(8,128)} %bitcast.8, ...), custom_call_target="tpu_custom_call" | custom-call | tf_op jit(solution)/shard_map/step/pallas_call | solution.py:469
  63.1 2.4 %finish.1 = (bf16[512,4096]{1,0:T(8,128)(2,1)}, f32[32,1024]{1,0:T(8,128)}, f32[1024,128]{1,0:T(8,128)}, f32[1024,128]{1,0:T(8,128)}) custom-call(bf16[512,4096]{1,0:T(8,128)(2,1)S(1)} %get-tuple-element.12.refs_0_, f32[32,1024]{1,0:T(8,128)S(1)} %get-tuple-element.13.refs_1_, f32[1024,128]{1,0:T(8,128)S(1)} %get-tuple-element.14.refs_2_, ...), custom_call_target="tpu_custom_call" | custom-call | tf_op jit(solution)/shard_map/finish/pallas_call | solution.py:518

commit v4 on v3

--- a/solution.py
+++ b/solution.py
@@ -228,11 +228,18 @@
     for dim in SIZES:
         peers += [towards(dim, sign) for sign, _ in arms(SIZES[dim], 0)]
 
+    half_width = xs.shape[1] // 2
+
+    def half_copy(n, sem):
+        columns = pl.ds(n * half_width, half_width)
+        return pltpu.make_async_copy(x_hbm.at[:, columns], xs.at[:, columns], sem)
+
     local = [
         pltpu.make_async_copy(w_hbm, w.at[at["z"], at["x"], at["y"], me_c], in_sem.at[0]),
         pltpu.make_async_copy(cot_hbm, cs, in_sem.at[1]),
+        half_copy(0, in_sem.at[2]),
+        half_copy(1, in_sem.at[6]),
         pltpu.make_async_copy(l_hbm, l, in_sem.at[3]),
-        pltpu.make_async_copy(x_hbm, xs, in_sem.at[2]),
         pltpu.make_async_copy(g_hbm, g, in_sem.at[4]),
         pltpu.make_async_copy(m_hbm, m, in_sem.at[5]),
     ]
@@ -349,8 +356,7 @@
             copy = remote(cs, pc, sw_s.at[planes], sw_r.at[planes], core)
             copy.start()
             swaps.append(copy)
-            local[2].wait()
-            local[3].wait()
+            local[4].wait()
         elif kind == "rep":
             hop1[event[1]].start()
         elif kind == "relay":
@@ -359,8 +365,8 @@
         elif kind == "outer":
             if kind not in done:
                 done.add(kind)
-                local[4].wait()
                 local[5].wait()
+                local[6].wait()
             hop2[event[1]].wait_recv()
             rows = pl.ds(event[1] * share, share)
             pseudo = g[rows] - (l[rows] + other[rows]) * 0.5
@@ -369,6 +375,9 @@
             ng[rows] = g[rows] - 0.7 * (pseudo + 0.9 * moment)
         elif kind == "xt":
             z = event[1]
+            if (kind, 2 * z // planes) not in done:
+                done.add((kind, 2 * z // planes))
+                local[2 + 2 * z // planes].wait()
             xt[z] = xs[:, z * width : (z + 1) * width].T.reshape(xt.shape[1:])
             copy = remote(xt.at[z, :, :, 1 - me_c], px.at[z], sw_s.at[z], sw_r.at[z], core)
             copy.start()
@@ -490,7 +499,7 @@
         + [pltpu.VMEM(flat, f32)] * 5
         + [pltpu.VMEM((nz, tok, d // nz), f32)]
         + [
-            dma((6,)),
+            dma((7,)),
             dma((n_ag,)),
             dma((n_ag,)),
             dma((PARTS,)),

time: 66.5 us -> 66.5 us (level)
  no operation moved by 1% of the time
where the time goes in v4:
time: 66.5 us; the launch traced here: 65.7 us
  Pallas kernels  64.9 us (98%)
  between operations  0.8 us (1%)
    pallas_call x1, Pallas kernels, shards(): pl.pallas_call(functools.partial(kernel, plan, factor), out_shape=(pltpu....  62.5 us
    pallas_call x1, Pallas kernels, shards(): pl.pallas_call(finish, out_shape=tuple((jax.ShapeDtypeStruct(o.shape, o.d...  2.41 us

profile of v4, /device:TPU:16, one launch (start us, length us, event | category | flops | bytes accessed | tf_op | source)
XLA Modules:
  0.0 65.7 jit_solution(3100887098886378527)
XLA Ops:
  0.6 62.5 %step.1 = (bf16[512,4096]{1,0:T(8,128)(2,1)S(1)}, f32[32,1024]{1,0:T(8,128)S(1)}, f32[1024,128]{1,0:T(8,128)S(1)}, f32[1024,128]{1,0:T(8,128)S(1)}) custom-call(bf16[512,4096]{1,0:T(8,128)(2,1)} %x_hbm.1, bf16[512,1024]{1,0:T(8,128)(2,1)} %cot_hbm.1, bf16[32,1024]{1,0:T(8,128)(2,1)} %bitcast.10, f32[1024,128]{1,0:T(8,128)} %bitcast.7, f32[1024,128]{1,0:T(8,128)} %bitcast.8, ...), custom_call_target="tpu_custom_call" | custom-call | tf_op jit(solution)/shard_map/step/pallas_call | solution.py:478
  63.1 2.4 %finish.1 = (bf16[512,4096]{1,0:T(8,128)(2,1)}, f32[32,1024]{1,0:T(8,128)}, f32[1024,128]{1,0:T(8,128)}, f32[1024,128]{1,0:T(8,128)}) custom-call(bf16[512,4096]{1,0:T(8,128)(2,1)S(1)} %get-tuple-element.12.refs_0_, f32[32,1024]{1,0:T(8,128)S(1)} %get-tuple-element.13.refs_1_, f32[1024,128]{1,0:T(8,128)S(1)} %get-tuple-element.14.refs_2_, ...), custom_call_target="tpu_custom_call" | custom-call | tf_op jit(solution)/shard_map/finish/pallas_call | solution.py:527
